TPU v7x, 128 devices: a whole 4x4x4 slice. The times are simulated.
128 devices in a mesh: dp: 4 (over z), mp: 32 (over y, x, core).
Axes of the slice: x: 4, y: 4, z: 4, core: 2. Of those that a mesh axis runs over, the one named last changes fastest.
Arguments:
- tokens: bfloat16 [4096, 4096], P('dp', 'mp'), may hold values from -6 to 6
- decay: float32 [4096, 16], P('dp'), may hold values from 0.75 to 1, as said below
- state: float32 [128, 256, 8192], P('dp', None, 'mp'), may hold values from -24 to 24
- w_query: bfloat16 [4096, 4096], P(None, 'mp'), may hold values from -0.09375 to 0.09375
- w_key: bfloat16 [4096, 4096], P(None, 'mp'), may hold values from -0.09375 to 0.09375
- w_value: bfloat16 [4096, 8192], P(None, 'mp'), may hold values from -0.09375 to 0.09375
- w_gate: bfloat16 [4096, 8192], P(None, 'mp'), may hold values from -0.09375 to 0.09375
- w_out: bfloat16 [8192, 4096], P('mp'), may hold values from -0.125 to 0.125
- norm_gain: float32 [8192], P('mp'), may hold values from 0.25 to 1.75
Outputs:
- layer_out: bfloat16 [4096, 4096], P('dp', 'mp')
- new_state: float32 [128, 256, 8192], P('dp', None, 'mp')
Inputs may be any that keep to these rules, and one draw needn't show every extreme that they name: `decay`: each head has its own base rate over all tokens, varied somewhat from token to token.
All inputs are finite; a program needn't handle non-finite values.
Results may differ from a plain program's by a relative error of at most 0.0071.
Values may be sent and summed in bfloat16 or wider, within the bound.
No kernel may reach another device: no remote copies, remote signals or barrier semaphores. Data moves between devices by JAX's collectives and lax.ppermute only.
A program may use at most 128 MiB of HBM per device.

v0:
```python
import jax
import jax.numpy as jnp
from jax import lax
from jax.sharding import PartitionSpec as P

HEAD = 256
VHEAD = 512
NEW = 32
EPS = 0.1


def partner(shard, axis, bit):
    return lax.ppermute(shard, axis, [(i, i ^ 1 << bit) for i in range(lax.axis_size(axis))])


def per_device(tokens, decay, state, w_query, w_key, w_value, w_gate, w_out, norm_gain):
    tok_rows = tokens.shape[0]
    qk_columns = w_query.shape[1]
    v_columns = w_value.shape[1]
    groups = max(1, qk_columns // HEAD)
    qk_width = qk_columns // groups
    v_width = v_columns // groups
    sequences = tok_rows // NEW
    device_index = lax.axis_index("mp")
    first_head = device_index * qk_columns // HEAD
    qk_zeros = jnp.zeros((tok_rows, qk_columns), jnp.float32)
    v_zeros = jnp.zeros((tok_rows, v_columns), jnp.float32)
    carried = (qk_zeros, qk_zeros, v_zeros, v_zeros)
    segment = lax.all_gather(tokens, "mp", axis=1, tiled=True)
    updated = []
    for running, weight in zip(carried, (w_query, w_key, w_value, w_gate)):
        weight_rows = weight
        updated.append(jnp.dot(segment, weight_rows, preferred_element_type=jnp.float32))
    query, key_proj, value_proj, gate_proj = tuple(updated)
    query = (query * HEAD ** (-0.5)).astype(jnp.bfloat16).reshape(tok_rows, groups, qk_width)
    key_proj = key_proj.astype(jnp.bfloat16).reshape(tok_rows, groups, qk_width)
    value_proj = value_proj.astype(jnp.bfloat16)
    bit_number = 0
    other_query, other_key = partner((query, key_proj), "mp", bit_number)
    upper_half = device_index >> bit_number & 1 == 1
    query = jnp.where(
        upper_half,
        jnp.concatenate([other_query, query], 2),
        jnp.concatenate([query, other_query], 2),
    )
    key_proj = jnp.where(
        upper_half,
        jnp.concatenate([other_key, key_proj], 2),
        jnp.concatenate([key_proj, other_key], 2),
    )
    query_block = query.reshape(sequences, NEW, groups, HEAD)
    key_block = key_proj.reshape(sequences, NEW, groups, HEAD)
    value_block = value_proj.reshape(sequences, NEW, groups, v_width)
    decay_rates = lax.dynamic_slice_in_dim(decay, first_head, groups, 1).reshape(
        sequences, NEW, groups
    )
    log_cumul = jnp.cumsum(jnp.log(decay_rates), axis=1)
    old_state = state.reshape(sequences, HEAD, groups, v_width)
    from_state = jnp.einsum("bngk,bkgv->bngv", query_block.astype(jnp.float32), old_state)
    scores = jnp.einsum(
        "bngk,bmgk->bgnm", query_block, key_block, preferred_element_type=jnp.float32
    )
    along = jnp.transpose(log_cumul, (0, 2, 1))
    log_gap = along[:, :, :, None] - along[:, :, None, :]
    causal = jnp.arange(NEW)[:, None] >= jnp.arange(NEW)[None, :]
    factor = jnp.where(causal, jnp.exp(jnp.where(causal, log_gap, 0.0)), 0.0)
    weights = (scores * factor).astype(jnp.bfloat16)
    in_block = jnp.einsum(
        "bgnm,bmgv->bngv", weights, value_block, preferred_element_type=jnp.float32
    )
    retained = jnp.exp(log_cumul)[..., None] * from_state + in_block
    final_log = log_cumul[:, -1, :]
    carry_scale = jnp.exp(final_log[:, None, :] - log_cumul)
    decayed_keys = key_block.astype(jnp.float32) * carry_scale[..., None]
    fresh = jnp.einsum("bngk,bngv->bkgv", decayed_keys, value_block.astype(jnp.float32))
    new_state = jnp.exp(final_log)[:, None, :, None] * old_state + fresh
    new_state = new_state.reshape(sequences, HEAD, v_columns)
    retained = retained.reshape(tok_rows, groups, v_width)
    running = jnp.sum(retained, axis=-1)
    squares = jnp.sum(retained * retained, axis=-1)
    bit_number = 0
    other_sum, other_square = partner((running, squares), "mp", bit_number)
    running = running + other_sum
    squares = squares + other_square
    centre = running / VHEAD
    variance = squares / VHEAD - centre * centre
    deviation = retained - centre[..., None]
    normed = deviation * lax.rsqrt(variance + EPS)[..., None]
    gated_out = (normed.reshape(tok_rows, v_columns) * norm_gain * jax.nn.silu(gate_proj)).astype(
        jnp.bfloat16
    )
    out_cols = lax.all_to_all(w_out, "mp", split_axis=1, concat_axis=0, tiled=True)
    weight_rows = out_cols
    layer_out = jnp.dot(
        lax.all_gather(gated_out, "mp", axis=1, tiled=True),
        weight_rows,
        preferred_element_type=jnp.float32,
    ).astype(jnp.bfloat16)
    return (layer_out, new_state)


def solution(mesh):
    placed = (
        P("dp", "mp"),
        P("dp", None),
        P("dp", None, "mp"),
        P(None, "mp"),
        P(None, "mp"),
        P(None, "mp"),
        P(None, "mp"),
        P("mp", None),
        P("mp"),
    )
    return jax.shard_map(
        per_device,
        mesh=mesh,
        in_specs=placed,
        out_specs=(P("dp", "mp"), P("dp", None, "mp")),
        check_vma=False,
    )
```

profile of v0, /device:TPU:1, one launch (start us, length us, event | category | flops | bytes accessed | tf_op | source)
XLA Modules:
  0.0 216.4 jit_solution(17912909884485674575)
XLA Ops:
  7.2 0.0 copy-start
  7.2 0.0 all-gather.3.cloned.1.call-start
  7.2 0.7 all-gather.3.cloned.1.call-update
  7.9 0.0 all-gather.5.cloned.1.call-start
  8.0 0.8 log_reduce_fusion
  8.8 0.1 log.15
  8.8 0.5 copy.22
  9.4 2.0 fusion.26
  11.4 0.4 copy.23
  11.7 0.1 slice_reduce_fusion
  11.9 0.1 subtract_exponential_fusion
  11.9 60.5 %all-gather.3.cloned.1.call-done = bf16[1024,4096]{1,0:T(8,128)(2,1)} async-done(((bf16[1024,128]{1,0:T(8,128)(2,1)}), bf16[1024,4096]{1,0:T(8,128)(2,1)}) %all-gather.3.cloned.1.call-update) | async-done | bytes 8388624 | tf_op jit(solution)/shard_map/all_gather | solution.py:29
  72.5 0.0 copy-start.10
  72.5 0.0 copy-start.11
  72.5 6.1 %fusion.4 = bf16[1024,128]{1,0:T(8,128)(2,1)S(1)} fusion(bf16[1024,4096]{1,0:T(8,128)(2,1)} %all-gather.3.cloned.1.call-done, bf16[4096,128]{1,0:T(8,128)(2,1)} %param.12), kind=kOutput, calls=%fused_computation.11 | convolution fusion | flops 1074003968 | bytes 9699328 | tf_op jit(solution)/shard_map/dot_general | solution.py:33
  78.5 0.3 collective-permute-start
  78.9 0.0 copy-done.10
  78.9 0.0 copy-done.11
  78.9 2.3 %convolution_convert_fusion.2 = bf16[1024,128]{1,0:T(8,128)(2,1)S(1)} fusion(bf16[1024,4096]{1,0:T(8,128)(2,1)S(1)} %copy-done.10, bf16[4096,128]{1,0:T(8,128)(2,1)S(1)} %copy-done.11), kind=kOutput, calls=%fused_computation.12 | convolution fusion | flops 1073872896 | bytes 9699328 | tf_op jit(solution)/shard_map/dot_general | solution.py:33
  81.2 0.0 copy-start.6
  81.2 0.3 collective-permute-start.1
  81.6 0.0 copy-done
  81.6 2.3 %convolution_convert_fusion = bf16[1024,256]{1,0:T(8,128)(2,1)S(1)} fusion(bf16[1024,4096]{1,0:T(8,128)(2,1)S(1)} %copy-done.10, bf16[4096,256]{1,0:T(8,128)(2,1)S(1)} %copy-done), kind=kOutput, calls=%fused_computation.6 | convolution fusion | flops 2147745792 | bytes 11010048 | tf_op jit(solution)/shard_map/dot_general | solution.py:33
  83.9 0.0 copy-start.3
  83.9 0.0 collective-permute-done
  83.9 0.0 copy-start.5
  83.9 0.0 collective-permute-done.1
  84.0 0.0 copy-start.8
  84.0 0.8 copy-done.8
  84.7 0.0 copy-start.12
  84.7 1.5 convolution_bitcast_fusion
  86.3 0.0 copy-done.6
  86.3 0.0 copy-done.3
  86.3 0.0 copy-done.5
  86.3 4.5 %fusion.9 = (f32[32,32]{1,0:T(8,128)S(1)}, f32[32,32]{1,0:T(8,128)S(1)}, f32[32,1,256,32]{2,3,0,1:T(8,128)S(1)}) fusion(f32[32,1,256,32]{2,3,0,1:T(8,128)S(1)} %convolution_bitcast_fusion, f32[32,256,256]{2,1,0:T(8,128)} %param.11, bf16[32,32,128]{2,1,0:T(8,128)(2,1)S(1)} %bitcast.72, bf16[32,32,128]{2,1,0:T(8,128)(2,1)} %bitcast.74, pred[]{:T(512)S(6)} %eq.3, ...), kind=kOutput, calls=%fused_computation.20 | convolution fusion | flops 137885696 | bytes 11022337 | tf_op jit(solution)/shard_map/bngk,bkgv->bngv/dot_general | solution.py:59
  90.8 0.1 reduce_sum.25
  90.9 0.1 reduce_sum.23
  91.0 0.3 collective-permute-start.2
  91.3 0.2 collective-permute-start.3
  91.5 0.7 collective-permute-done.2
  92.2 0.3 collective-permute-done.3
  92.5 0.0 copy-done.12
  92.5 0.0 copy-start.2
  92.5 7.4 %fusion.8 = bf16[1024,256]{1,0:T(8,128)(2,1)} fusion(f32[32,1,256,32]{2,3,0,1:T(8,128)S(1)} %get-tuple-element.14, f32[256]{0:T(256)S(1)} %copy-done.12, f32[1024]{0:T(1024)S(1)} %bitcast.81, f32[1024]{0:T(1024)S(1)} %bitcast.82, bf16[1024,4096]{1,0:T(8,128)(2,1)} %all-gather.3.cloned.1.call-done, bf16[4096,256]{1,0:T(8,128)(2,1)} %param.15), kind=kOutput, calls=%fused_computation.17 | convolution fusion | flops 2149842944 | bytes 12067840 | tf_op jit(solution)/shard_map/dot_general | solution.py:33
  99.9 0.0 all-gather.5.cloned.1.call-update
  99.9 0.0 copy-done.2
  99.9 2.5 %copy.24 = bf16[256,4096]{0,1:T(8,128)(2,1)} copy(bf16[256,4096]{1,0:T(8,128)(2,1)S(1)} %copy-done.2) | data formatting | bytes 4194304 | tf_op args[7]
  102.4 5.6 %all-to-all-start = ((bf16[256,32,128]{0,2,1:T(8,128)(2,1)}), bf16[256,32,128]{0,2,1:T(8,128)(2,1)S(1)}, u32[]{:S(2)}, u32[]{:S(2)}) async-start(bf16[256,32,128]{0,2,1:T(8,128)(2,1)} %bitcast.66), calls=%async_computation | async-start | bytes 4194304 | tf_op jit(solution)/shard_map/all_to_all | solution.py:92
  108.0 0.0 copy-start.4
  108.0 0.0 copy-start.7
  108.0 0.0 copy-start.9
  108.0 9.2 %copy.26 = f32[32,256,256]{1,2,0:T(8,128)} copy(f32[32,256,256]{2,1,0:T(8,128)} %param.11) | data formatting | bytes 16777216 | tf_op args[2]
  117.2 27.7 %all-to-all-done = bf16[256,32,128]{0,2,1:T(8,128)(2,1)S(1)} async-done(((bf16[256,32,128]{0,2,1:T(8,128)(2,1)}), bf16[256,32,128]{0,2,1:T(8,128)(2,1)S(1)}, u32[]{:S(2)}, u32[]{:S(2)}) %all-to-all-start) | async-done | bytes 2097184 | tf_op jit(solution)/shard_map/all_to_all | solution.py:92
  144.9 2.9 %copy.25 = bf16[32,256,128]{2,1,0:T(8,128)(2,1)} copy(bf16[32,256,128]{1,2,0:T(8,128)(2,1)S(1)} %bitcast.65) | data formatting | bytes 4194304 | tf_op jit(solution)/shard_map/all_to_all | solution.py:92
  147.8 0.0 copy-done.4
  147.8 0.0 copy-done.7
  147.8 0.0 copy-done.9
  147.8 8.5 %fusion = f32[32,256,256]{1,2,0:T(8,128)} fusion(f32[32,256,256]{1,2,0:T(8,128)} %copy.26, f32[32]{0:T(128)S(1)} %exp.38, bf16[32,32,256]{2,1,0:T(8,128)(2,1)S(1)} %bitcast.69, f32[32,32]{1,0:T(8,128)S(1)} %get-tuple-element.12, bf16[32,32,128]{2,1,0:T(8,128)(2,1)S(1)} %bitcast.77, bf16[32,32,128]{2,1,0:T(8,128)(2,1)S(1)} %bitcast.79, pred[]{:T(512)S(6)} %eq.3), kind=kOutput, calls=%fused_computation.1 | convolution fusion | flops 141295616 | bytes 17830016 | tf_op jit(solution)/shard_map/bngk,bngv->bkgv/dot_general | solution.py:75
  156.3 9.0 %copy.27 = f32[32,256,256]{2,1,0:T(8,128)} copy(f32[32,256,256]{1,2,0:T(8,128)} %fusion) | data formatting | bytes 16777216
  165.3 32.6 %all-gather.5.cloned.1.call-done = bf16[1024,8192]{1,0:T(8,128)(2,1)} async-done(((bf16[1024,256]{1,0:T(8,128)(2,1)}), bf16[1024,8192]{1,0:T(8,128)(2,1)}) %all-gather.5.cloned.1.call-update) | async-done | bytes 16777232 | tf_op jit(solution)/shard_map/all_gather | solution.py:95
  197.9 0.0 copy-start.1
  197.9 11.7 %convolution_convert_fusion.1 = bf16[1024,128]{1,0:T(8,128)(2,1)} fusion(bf16[1024,8192]{1,0:T(8,128)(2,1)} %all-gather.5.cloned.1.call-done, bf16[8192,128]{1,0:T(8,128)(2,1)} %bitcast.67), kind=kOutput, calls=%fused_computation.9 | convolution fusion | flops 2147614720 | bytes 19136512 | tf_op jit(solution)/shard_map/dot_general | solution.py:94
  209.6 0.0 copy-done.1
  (3 shorter events, 0.0 us)
Async XLA Ops:
  7.2 74.4 %copy-start = (bf16[4096,256]{1,0:T(8,128)(2,1)S(1)}, bf16[4096,256]{1,0:T(8,128)(2,1)}, u32[]{:S(2)}) copy-start(bf16[4096,256]{1,0:T(8,128)(2,1)} %param.14) | copy-start | bytes 6291460
  7.2 65.3 %all-gather.3.cloned.1.call-start = ((), (), s32[]{:S(2)}) async-start(), calls=%async_computation.1 | async-start | bytes 8650752 | tf_op jit(solution)/shard_map/all_gather | solution.py:29
  7.9 190.0 %all-gather.5.cloned.1.call-start = ((), (), s32[]{:S(2)}) async-start(), calls=%async_computation.2 | async-start | bytes 17301504 | tf_op jit(solution)/shard_map/all_gather | solution.py:95
  72.5 6.4 %copy-start.10 = (bf16[1024,4096]{1,0:T(8,128)(2,1)S(1)}, bf16[1024,4096]{1,0:T(8,128)(2,1)}, u32[]{:S(2)}) copy-start(bf16[1024,4096]{1,0:T(8,128)(2,1)} %all-gather.3.cloned.1.call-done) | copy-start | bytes 25165828
  72.5 6.4 %copy-start.11 = (bf16[4096,128]{1,0:T(8,128)(2,1)S(1)}, bf16[4096,128]{1,0:T(8,128)(2,1)}, u32[]{:S(2)}) copy-start(bf16[4096,128]{1,0:T(8,128)(2,1)} %param.13) | copy-start | bytes 3145732
  78.5 5.4 %collective-permute-start = (bf16[1024,1,128]{2,0,1:T(8,128)(2,1)S(1)}, bf16[1024,1,128]{2,0,1:T(8,128)(2,1)S(1)}, u32[]{:S(2)}, u32[]{:S(2)}) collective-permute-start(bf16[1024,1,128]{2,0,1:T(8,128)(2,1)S(1)} %bitcast.70), channel_id=1, source_target_pairs={{0,1},{1,0},{2,3},{3,2},{4,5},{5,4},{6,7},{7,6},{8,9},{9,8},{10,11... | collective-permute-start | bytes 786440 | tf_op jit(solution)/shard_map/ppermute | solution.py:13
  81.2 5.0 %copy-start.6 = (bf16[1024,128]{1,0:T(8,128)(2,1)}, bf16[1024,128]{1,0:T(8,128)(2,1)S(1)}, u32[]{:S(2)}) copy-start(bf16[1024,128]{1,0:T(8,128)(2,1)S(1)} %convolution_convert_fusion.2) | copy-start | bytes 786436
  81.2 2.7 %collective-permute-start.1 = (bf16[1024,1,128]{2,0,1:T(8,128)(2,1)S(1)}, bf16[1024,1,128]{2,0,1:T(8,128)(2,1)S(1)}, u32[]{:S(2)}, u32[]{:S(2)}) collective-permute-start(bf16[1024,1,128]{2,0,1:T(8,128)(2,1)S(1)} %bitcast.75), channel_id=1, source_target_pairs={{0,1},{1,0},{2,3},{3,2},{4,5},{5,4},{6,7},{7,6},{8,9},{9,8},{10,11... | collective-permute-start | bytes 786440 | tf_op jit(solution)/shard_map/ppermute | solution.py:13
  83.9 2.4 %copy-start.3 = (bf16[1024,256]{1,0:T(8,128)(2,1)}, bf16[1024,256]{1,0:T(8,128)(2,1)S(1)}, u32[]{:S(2)}) copy-start(bf16[1024,256]{1,0:T(8,128)(2,1)S(1)} %convolution_convert_fusion) | copy-start | bytes 1572868
  83.9 2.4 %copy-start.5 = (bf16[1024,1,128]{2,0,1:T(8,128)(2,1)}, bf16[1024,1,128]{2,0,1:T(8,128)(2,1)S(1)}, u32[]{:S(2)}) copy-start(bf16[1024,1,128]{2,0,1:T(8,128)(2,1)S(1)} %collective-permute-done) | copy-start | bytes 786436
  84.0 0.8 copy-start.8
  84.7 7.8 %copy-start.12 = (f32[256]{0:T(256)S(1)}, f32[256]{0:T(256)}, u32[]{:S(2)}) copy-start(f32[256]{0:T(256)} %param.17) | copy-start | bytes 3076
  91.0 1.2 collective-permute-start.2
  91.3 1.2 collective-permute-start.3
  92.5 7.4 %copy-start.2 = (bf16[256,4096]{1,0:T(8,128)(2,1)S(1)}, bf16[256,4096]{1,0:T(8,128)(2,1)}, u32[]{:S(2)}) copy-start(bf16[256,4096]{1,0:T(8,128)(2,1)} %param.16) | copy-start | bytes 6291460
  102.4 42.5 %all-to-all-start = ((bf16[256,32,128]{0,2,1:T(8,128)(2,1)}), bf16[256,32,128]{0,2,1:T(8,128)(2,1)S(1)}, u32[]{:S(2)}, u32[]{:S(2)}) async-start(bf16[256,32,128]{0,2,1:T(8,128)(2,1)} %bitcast.66), calls=%async_computation | async-start | bytes 4194304 | tf_op jit(solution)/shard_map/all_to_all | solution.py:92
  108.0 39.8 %copy-start.4 = (bf16[1024,256]{1,0:T(8,128)(2,1)S(1)}, bf16[1024,256]{1,0:T(8,128)(2,1)}, u32[]{:S(2)}) copy-start(bf16[1024,256]{1,0:T(8,128)(2,1)} %copy-done.3) | copy-start | bytes 1572868
  108.0 39.8 %copy-start.7 = (bf16[1024,128]{1,0:T(8,128)(2,1)S(1)}, bf16[1024,128]{1,0:T(8,128)(2,1)}, u32[]{:S(2)}) copy-start(bf16[1024,128]{1,0:T(8,128)(2,1)} %copy-done.6) | copy-start | bytes 786436
  108.0 39.8 %copy-start.9 = (bf16[1024,1,128]{2,0,1:T(8,128)(2,1)S(1)}, bf16[1024,1,128]{2,0,1:T(8,128)(2,1)}, u32[]{:S(2)}) copy-start(bf16[1024,1,128]{2,0,1:T(8,128)(2,1)} %copy-done.8) | copy-start | bytes 786436
  197.9 11.7 %copy-start.1 = (bf16[4096,256]{1,0:T(8,128)(2,1)S(1)}, bf16[4096,256]{1,0:T(8,128)(2,1)}, u32[]{:S(2)}) copy-start(bf16[4096,256]{1,0:T(8,128)(2,1)} %param.14) | copy-start | bytes 6291460
Sparse Core Ops, SparseCore 0:
  10.2 62.2 all-gather.2
  100.0 97.8 all-gather.4
where the time goes:
time: 217 us; the launch traced here: 216 us
  waiting for transfers between devices  122 us (56%)
  matrix products  44.4 us (20%)
  local copies, waits for them, and re-layouts  26.4 us (12%)
  between operations  14.3 us (7%)
  starting transfers between devices  6.87 us (3%)
    all_gather x1, waiting for transfers between devices, per_device(): segment = lax.all_gather(tokens, 'mp', axis=1, tiled=True)  60.5 us
    all_gather x1, waiting for transfers between devices, per_device(): lax.all_gather(gated_out, 'mp', axis=1, tiled=True)  32.6 us
    all_to_all x1, waiting for transfers between devices, per_device(): lax.all_to_all(w_out, 'mp', split_axis=1, concat_axis=0, tiled=True)  27.7 us
    unnamed x29, local copies, waits for them, and re-layouts  21.5 us
    dot_general x4, matrix products, per_device(): jnp.dot(segment, weight_rows, preferred_element_type=jnp.float32)  18.1 us
    dot_general x1, matrix products, per_device(): jnp.dot(lax.all_gather(gated_out, 'mp', axis=1, tiled=True), weight_rows,...  11.7 us
    dot_general x1, matrix products, per_device(): jnp.einsum('bngk,bngv->bkgv', decayed_keys, value_block.astype(jnp.float32))  8.48 us
    all_to_all x1, starting transfers between devices, per_device(): lax.all_to_all(w_out, 'mp', split_axis=1, concat_axis=0, tiled=True)  5.6 us
  transfers between devices with their start and end apart: 7, of which 5 were waited for; matrix products, arithmetic and copies ran while one was open for 19% of the time, Pallas kernels for 0%

commit v1 on v0

--- a/solution.py
+++ b/solution.py
@@ -92,7 +92,9 @@
     out_cols = lax.all_to_all(w_out, "mp", split_axis=1, concat_axis=0, tiled=True)
     weight_rows = out_cols
     layer_out = jnp.dot(
-        lax.all_gather(gated_out, "mp", axis=1, tiled=True),
+        jnp.concatenate(
+            lax.all_to_all(jnp.stack([gated_out] * lax.axis_size("mp")), "mp", 0, 0), axis=1
+        ),
         weight_rows,
         preferred_element_type=jnp.float32,
     ).astype(jnp.bfloat16)

time: 217 us -> 360 us (1.66)
  the two profiles are of different devices: /device:TPU:1 before, /device:TPU:0 now
where the time goes in v1:
time: 360 us; the launch traced here: 359 us
  waiting for transfers between devices  250 us (69%)
  matrix products  42.6 us (12%)
  local copies, waits for them, and re-layouts  34.9 us (10%)
  starting transfers between devices  14.7 us (4%)
  between operations  14.2 us (4%)
    all_to_all x1, waiting for transfers between devices, per_device(): lax.all_to_all(jnp.stack([gated_out] * lax.axis_size('mp')), 'mp', 0, 0)  187 us
    all_gather x1, waiting for transfers between devices, per_device(): segment = lax.all_gather(tokens, 'mp', axis=1, tiled=True)  61.6 us
    unnamed x17, local copies, waits for them, and re-layouts  22.9 us
    dot_general x4, matrix products, per_device(): jnp.dot(segment, weight_rows, preferred_element_type=jnp.float32)  17.2 us
    dot_general x1, matrix products, per_device(): jnp.dot(jnp.concatenate(lax.all_to_all(jnp.stack([gated_out] * lax.axis_s...  11.6 us
    dot_general x1, matrix products, per_device(): jnp.einsum('bngk,bngv->bkgv', decayed_keys, value_block.astype(jnp.float32))  7.98 us
    all_to_all x1, starting transfers between devices, per_device(): lax.all_to_all(w_out, 'mp', split_axis=1, concat_axis=0, tiled=True)  7.56 us
  transfers between devices with their start and end apart: 7, of which 4 were waited for; matrix products, arithmetic and copies ran while one was open for 17% of the time, Pallas kernels for 0%

profile of v1, /device:TPU:0, one launch (start us, length us, event | category | flops | bytes accessed | tf_op | source)
XLA Modules:
  0.0 358.9 jit_solution(11488868237713420716)
XLA Ops:
  7.2 0.0 copy-start
  7.2 0.0 all-gather.2.cloned.1.call-start
  7.2 0.7 all-gather.2.cloned.1.call-update
  7.9 4.1 %copy.20 = bf16[256,4096]{0,1:T(8,128)(2,1)} copy(bf16[256,4096]{1,0:T(8,128)(2,1)} %param.16) | data formatting | bytes 4194304 | tf_op args[7]
  12.0 4.1 %copy.21 = bf16[256,32,128]{2,0,1:T(8,128)(2,1)} copy(bf16[256,32,128]{0,2,1:T(8,128)(2,1)} %bitcast.79) | data formatting | bytes 4194304 | tf_op jit(solution)/shard_map/all_to_all | solution.py:92
  16.0 7.6 %all-to-all-start.1 = ((bf16[256,32,128]{2,0,1:T(8,128)(2,1)}), bf16[256,32,128]{2,0,1:T(8,128)(2,1)}, u32[]{:S(2)}, u32[]{:S(2)}) async-start(bf16[256,32,128]{2,0,1:T(8,128)(2,1)} %copy.21), calls=%async_computation.1 | async-start | bytes 4194304 | tf_op jit(solution)/shard_map/all_to_all | solution.py:92
  23.6 0.8 log_reduce_fusion
  24.4 0.1 log.15
  24.5 0.5 copy.18
  25.0 2.0 fusion.39
  27.0 0.4 copy.19
  27.4 0.1 slice_reduce_fusion
  27.5 0.1 subtract_exponential_fusion
  27.6 61.6 %all-gather.2.cloned.1.call-done = bf16[1024,4096]{1,0:T(8,128)(2,1)} async-done(((bf16[1024,128]{1,0:T(8,128)(2,1)}), bf16[1024,4096]{1,0:T(8,128)(2,1)}) %all-gather.2.cloned.1.call-update) | async-done | bytes 8388624 | tf_op jit(solution)/shard_map/all_gather | solution.py:29
  89.2 0.0 copy-start.4
  89.2 0.0 copy-start.5
  89.2 6.1 %convolution_convert_fusion.1 = bf16[1024,128]{1,0:T(8,128)(2,1)S(1)} fusion(bf16[1024,4096]{1,0:T(8,128)(2,1)} %all-gather.2.cloned.1.call-done, bf16[4096,128]{1,0:T(8,128)(2,1)} %param.13), kind=kOutput, calls=%fused_computation.15 | convolution fusion | flops 1073872896 | bytes 9699328 | tf_op jit(solution)/shard_map/dot_general | solution.py:33
  95.3 0.3 collective-permute-start.1
  95.6 0.0 copy-done.4
  95.6 0.0 copy-done.5
  95.6 2.3 fusion.12
  97.9 0.3 collective-permute-start
  98.3 0.0 copy-done
  98.3 2.3 convolution_convert_fusion
  100.6 0.0 collective-permute-done.1
  100.6 0.0 copy-start.2
  100.6 0.0 collective-permute-done
  100.6 0.7 copy-done.2
  101.3 0.0 copy-start.6
  101.3 1.6 convolution_bitcast_fusion
  102.9 4.4 %fusion.22 = (f32[32,32]{1,0:T(8,128)S(1)}, f32[32,32]{1,0:T(8,128)S(1)}, f32[32,1,256,32]{2,3,0,1:T(8,128)S(1)}) fusion(f32[32,1,256,32]{2,3,0,1:T(8,128)S(1)} %convolution_bitcast_fusion, f32[32,256,256]{2,1,0:T(8,128)} %param.11, bf16[32,32,128]{2,1,0:T(8,128)(2,1)S(1)} %bitcast.84, bf16[32,32,128]{2,1,0:T(8,128)(2,1)S(1)} %bitcast.86, pred[]{:T(512)S(6)} %eq.3, ...), kind=kOutput, calls=%fused_computation.24 | convolution fusion | flops 137885696 | bytes 11022337 | tf_op jit(solution)/shard_map/bngk,bkgv->bngv/dot_general | solution.py:59
  107.3 0.1 reduce_sum.25
  107.3 0.3 collective-permute-start.3
  107.6 0.1 reduce_sum.23
  107.7 0.5 collective-permute-start.2
  108.1 0.4 collective-permute-done.3
  108.5 0.5 collective-permute-done.2
  109.1 0.0 copy-done.6
  109.1 6.4 %fusion.21 = bf16[1024,256]{1,0:T(8,128)(2,1)S(1)} fusion(f32[32,1,256,32]{2,3,0,1:T(8,128)S(1)} %get-tuple-element.12, f32[256]{0:T(256)S(1)} %copy-done.6, f32[1024]{0:T(1024)S(1)} %bitcast.93, f32[1024]{0:T(1024)S(1)} %bitcast.94, bf16[1024,4096]{1,0:T(8,128)(2,1)} %all-gather.2.cloned.1.call-done, bf16[4096,256]{1,0:T(8,128)(2,1)} %param.15), kind=kOutput, calls=%fused_computation.21 | convolution fusion | flops 2149842944 | bytes 12067840 | tf_op jit(solution)/shard_map/dot_general | solution.py:33
  115.5 0.0 all-to-all-done.1
  115.5 6.0 %stack.2 = bf16[32,1024,256]{2,1,0:T(8,128)(2,1)} broadcast(bf16[1024,256]{1,0:T(8,128)(2,1)S(1)} %fusion.21), dimensions={1,2} | broadcast | bytes 17301504 | tf_op jit(solution)/shard_map/stack | solution.py:96
  121.5 5.7 %all-to-all-start = ((bf16[32,1024,256]{2,1,0:T(8,128)(2,1)}), bf16[32,1024,256]{2,1,0:T(8,128)(2,1)}, u32[]{:S(2)}, u32[]{:S(2)}) async-start(bf16[32,1024,256]{2,1,0:T(8,128)(2,1)} %stack.2), calls=%async_computation | async-start | bytes 33554432 | tf_op jit(solution)/shard_map/all_to_all | solution.py:96
  127.2 0.0 copy-start.3
  127.2 9.0 %copy.22 = f32[32,256,256]{1,2,0:T(8,128)} copy(f32[32,256,256]{2,1,0:T(8,128)} %param.11) | data formatting | bytes 16777216 | tf_op args[2]
  136.2 0.0 copy-done.3
  136.2 8.0 %fusion.2 = f32[32,256,256]{1,2,0:T(8,128)} fusion(f32[32,256,256]{1,2,0:T(8,128)} %copy.22, f32[32]{0:T(128)S(1)} %exp.38, bf16[32,32,256]{2,1,0:T(8,128)(2,1)S(1)} %bitcast.81, f32[32,32]{1,0:T(8,128)S(1)} %get-tuple-element.10, bf16[32,32,128]{2,1,0:T(8,128)(2,1)S(1)} %bitcast.89, bf16[32,32,128]{2,1,0:T(8,128)(2,1)S(1)} %bitcast.91, pred[]{:T(512)S(6)} %eq.3), kind=kOutput, calls=%fused_computation.3 | convolution fusion | flops 141295616 | bytes 17830016 | tf_op jit(solution)/shard_map/bngk,bngv->bkgv/dot_general | solution.py:75
  144.2 0.0 copy-start.1
  144.2 9.1 %copy.23 = f32[32,256,256]{2,1,0:T(8,128)} copy(f32[32,256,256]{1,2,0:T(8,128)} %fusion.2) | data formatting | bytes 16777216
  153.3 187.2 %all-to-all-done = bf16[32,1024,256]{2,1,0:T(8,128)(2,1)} async-done(((bf16[32,1024,256]{2,1,0:T(8,128)(2,1)}), bf16[32,1024,256]{2,1,0:T(8,128)(2,1)}, u32[]{:S(2)}, u32[]{:S(2)}) %all-to-all-start) | async-done | bytes 16777248 | tf_op jit(solution)/shard_map/all_to_all | solution.py:96
  340.5 11.6 %fusion.13 = bf16[1024,128]{1,0:T(8,128)(2,1)} fusion(bf16[256,32,128]{2,0,1:T(8,128)(2,1)} %all-to-all-done.1, bf16[32,1024,256]{2,1,0:T(8,128)(2,1)} %all-to-all-done), kind=kOutput, calls=%fused_computation.16 | convolution fusion | flops 2147614720 | bytes 19136512 | tf_op jit(solution)/shard_map/dot_general | solution.py:94
  352.0 0.0 copy-done.1
  (3 shorter events, 0.0 us)
Async XLA Ops:
  7.2 91.1 %copy-start = (bf16[4096,256]{1,0:T(8,128)(2,1)S(1)}, bf16[4096,256]{1,0:T(8,128)(2,1)}, u32[]{:S(2)}) copy-start(bf16[4096,256]{1,0:T(8,128)(2,1)} %param.14) | copy-start | bytes 6291460
  7.2 82.0 %all-gather.2.cloned.1.call-start = ((), (), s32[]{:S(2)}) async-start(), calls=%async_computation.2 | async-start | bytes 8650752 | tf_op jit(solution)/shard_map/all_gather | solution.py:29
  16.0 99.5 %all-to-all-start.1 = ((bf16[256,32,128]{2,0,1:T(8,128)(2,1)}), bf16[256,32,128]{2,0,1:T(8,128)(2,1)}, u32[]{:S(2)}, u32[]{:S(2)}) async-start(bf16[256,32,128]{2,0,1:T(8,128)(2,1)} %copy.21), calls=%async_computation.1 | async-start | bytes 4194304 | tf_op jit(solution)/shard_map/all_to_all | solution.py:92
  89.2 6.4 %copy-start.4 = (bf16[1024,4096]{1,0:T(8,128)(2,1)S(1)}, bf16[1024,4096]{1,0:T(8,128)(2,1)}, u32[]{:S(2)}) copy-start(bf16[1024,4096]{1,0:T(8,128)(2,1)} %all-gather.2.cloned.1.call-done) | copy-start | bytes 25165828
  89.2 6.4 %copy-start.5 = (bf16[4096,128]{1,0:T(8,128)(2,1)S(1)}, bf16[4096,128]{1,0:T(8,128)(2,1)}, u32[]{:S(2)}) copy-start(bf16[4096,128]{1,0:T(8,128)(2,1)} %param.12) | copy-start | bytes 3145732
  95.3 5.4 %collective-permute-start.1 = (bf16[1024,1,128]{2,0,1:T(8,128)(2,1)S(1)}, bf16[1024,1,128]{2,0,1:T(8,128)(2,1)S(1)}, u32[]{:S(2)}, u32[]{:S(2)}) collective-permute-start(bf16[1024,1,128]{2,0,1:T(8,128)(2,1)S(1)} %bitcast.87), channel_id=1, source_target_pairs={{0,1},{1,0},{2,3},{3,2},{4,5},{5,4},{6,7},{7,6},{8,9},{9,8},{10,11... | collective-permute-start | bytes 786440 | tf_op jit(solution)/shard_map/ppermute | solution.py:13
  97.9 2.7 collective-permute-start
  100.6 0.7 copy-start.2
  101.3 7.7 %copy-start.6 = (f32[256]{0:T(256)S(1)}, f32[256]{0:T(256)}, u32[]{:S(2)}) copy-start(f32[256]{0:T(256)} %param.17) | copy-start | bytes 3076
  107.3 1.2 collective-permute-start.3
  107.7 1.4 collective-permute-start.2
  121.5 219.0 %all-to-all-start = ((bf16[32,1024,256]{2,1,0:T(8,128)(2,1)}), bf16[32,1024,256]{2,1,0:T(8,128)(2,1)}, u32[]{:S(2)}, u32[]{:S(2)}) async-start(bf16[32,1024,256]{2,1,0:T(8,128)(2,1)} %stack.2), calls=%async_computation | async-start | bytes 33554432 | tf_op jit(solution)/shard_map/all_to_all | solution.py:96
  127.2 9.0 %copy-start.3 = (bf16[1024,1,128]{2,0,1:T(8,128)(2,1)S(1)}, bf16[1024,1,128]{2,0,1:T(8,128)(2,1)}, u32[]{:S(2)}) copy-start(bf16[1024,1,128]{2,0,1:T(8,128)(2,1)} %copy-done.2) | copy-start | bytes 786436
  144.2 207.8 %copy-start.1 = (bf16[4096,256]{1,0:T(8,128)(2,1)S(1)}, bf16[4096,256]{1,0:T(8,128)(2,1)}, u32[]{:S(2)}) copy-start(bf16[4096,256]{1,0:T(8,128)(2,1)} %param.14) | copy-start | bytes 6291460
Sparse Core Ops, SparseCore 0:
  10.2 78.9 all-gather.1
